TPU v7x, 32 devices: a whole 2x2x4 slice. The times are simulated.
32 devices in a mesh: dev: 32 (over z, y, x, core).
Axes of the slice: x: 2, y: 2, z: 4, core: 2. Of those that a mesh axis runs over, the one named last changes fastest.
Arguments:
- state_real: float32 [4194304], P('dev'), may hold values from -24 to 24, as said below
- state_imag: float32 [4194304], P('dev'), may hold values from -24 to 24, as said below
- subsystem: int32 [3], replicated, may hold values from 0 to 16, as said below
Outputs:
- rho_real: float32 [256, 256], P('dev')
- rho_imag: float32 [256, 256], P('dev')
Inputs may be any that keep to these rules, and one draw needn't show every extreme that they name: `subsystem`: the 3 entries are distinct local bit positions in ascending order; the first is always 0 and the last always 17 - 1. `state_real`: real parts of amplitudes; their typical size changes between aligned blocks of 2**(11) local indices by up to a factor of 16. `state_imag`: imaginary parts of amplitudes, with the same block sizes as the real parts.
All inputs are finite; a program needn't handle non-finite values.
Results may differ from a plain program's by a relative error of at most 0.0001.
Values sent between devices are 32-bit elements; how exact they have to be, the bound alone decides.
A program may use at most 192 MiB of HBM per device.

v0:
```python
import jax
import jax.numpy as jnp
from jax import lax
from jax.sharding import PartitionSpec as P


def regroup(local_bits):
    branches = []
    for lower_count in range(local_bits - 2):

        def make_branch(flat, lower_count=lower_count):
            upper = 2 ** (local_bits - 3 - lower_count)
            lower = 2**lower_count
            shaped = flat.reshape(2, upper, 2, lower, 2)
            moved = jnp.transpose(shaped, (0, 2, 4, 1, 3))
            return moved.reshape(8, upper * lower)

        branches.append(make_branch)
    return branches


def contract(left, right):
    return lax.dot_general(
        left,
        right,
        (((1,), (1,)), ((), ())),
        precision=lax.Precision.HIGHEST,
        preferred_element_type=jnp.float32,
    )


def gram(left_re, left_im, right_re, right_im):
    joined = jnp.concatenate([right_re, right_im], axis=1)
    left_x = jnp.concatenate([left_re, left_im], axis=1)
    left_y = jnp.concatenate([left_im, -left_re], axis=1)
    product = contract(jnp.concatenate([left_x, left_y], axis=0), joined)
    row_total = left_re.shape[0]
    return (product[:row_total], product[row_total:])


def local(state_real, state_imag, subsystem):
    local_bits = state_real.shape[0].bit_length() - 1
    count_rest = state_real.shape[0] // 8
    branches = regroup(local_bits)
    middle_place = jnp.clip(subsystem[1] - 1, 0, local_bits - 3)
    local_real = lax.switch(middle_place, branches, state_real)
    local_imag = lax.switch(middle_place, branches, state_imag)
    received_re, received_im = (
        lax.all_to_all(local_real, "dev", split_axis=1, concat_axis=0, tiled=True),
        lax.all_to_all(local_imag, "dev", split_axis=1, concat_axis=0, tiled=True),
    )
    full_width = received_re.shape[0]
    scale = 1.0 / count_rest
    left_re = lax.slice_in_dim(received_re, 0, full_width, axis=0)
    left_im = lax.slice_in_dim(received_im, 0, full_width, axis=0)
    real_part, imag_part = gram(left_re, left_im, received_re, received_im)
    own_rows = lax.psum_scatter(
        jnp.concatenate([real_part, imag_part], axis=1), "dev", scatter_dimension=0, tiled=True
    )
    own_rows = own_rows * scale
    return (own_rows[:, :full_width], own_rows[:, full_width:])


def solution(mesh):
    return jax.shard_map(
        local,
        mesh=mesh,
        in_specs=(P("dev"), P("dev"), P()),
        out_specs=(P("dev", None), P("dev", None)),
        check_vma=False,
    )
```

profile of v0, /device:TPU:0, one launch (start us, length us, event | category | flops | bytes accessed | tf_op | source)
XLA Modules:
  0.0 324.3 jit_solution(1908655987549556454)
XLA Ops:
  7.2 1.2 slice.15
  9.1 0.0 copy-start
  9.1 69.1 %conditional.2 = (f32[8,16384]{1,0:T(8,128)}) conditional(s32[]{:T(128)} %bitcast.30, f32[131072]{0:T(1024)} %param.33, f32[131072]{0:T(1024)} %param.33, f32[131072]{0:T(1024)} %param.33, f32[131072]{0:T(1024)} %param.33, f32[131072]{0:T(1024)} %param.33, f32[131072]{0:T(1024)} %param.33, ...), branch_computations={%region_0.1_spmd, %region_1.2_spmd, %region_2.3_spmd, %region_3.4_... | conditional | bytes 3145736 | solution.py:46
  17.4 35.6 %reshape.153 = f32[2,128,2,128,2]{4,3,2,1,0:T(8,128)} reshape(f32[131072]{0:T(1024)} %param.7) | data formatting | bytes 1048576 | tf_op jit(solution)/shard_map/cond/branch_7_fun/reshape | solution.py:14
  53.0 19.5 %copy.60 = f32[2,2,2,128,128]{4,3,2,1,0:T(8,128)S(1)} copy(f32[2,2,2,128,128]{2,4,1,3,0:T(8,128)} %bitcast.127) | data formatting | bytes 1048576 | tf_op jit(solution)/shard_map/cond/branch_7_fun/transpose | solution.py:15
  72.4 1.1 copy.103
  78.2 0.0 copy-done
  78.2 7.5 %all-to-all-start = ((f32[8,32,512]{2,0,1:T(8,128)}), f32[8,32,512]{2,0,1:T(8,128)}, u32[]{:S(2)}, u32[]{:S(2)}) async-start(f32[8,32,512]{2,0,1:T(8,128)} %bitcast.31), calls=%async_computation | async-start | bytes 1048576 | tf_op jit(solution)/shard_map/all_to_all | solution.py:49
  85.7 67.4 %conditional.3 = (f32[8,16384]{1,0:T(8,128)}) conditional(s32[]{:T(128)} %bitcast.30, f32[131072]{0:T(1024)S(1)} %copy-done, f32[131072]{0:T(1024)S(1)} %copy-done, f32[131072]{0:T(1024)S(1)} %copy-done, f32[131072]{0:T(1024)S(1)} %copy-done, f32[131072]{0:T(1024)S(1)} %copy-done, f32[131072]{0:T(1024)S(1)} %copy-done, ...), branch_computations={%region_15.16_spmd, %region_16.17_spmd, %region_17.18_spmd, %regio... | conditional | bytes 3145736 | solution.py:47
  94.8 34.8 %reshape.183 = f32[2,128,2,128,2]{4,3,2,1,0:T(8,128)} reshape(f32[131072]{0:T(1024)S(1)} %param.22) | data formatting | bytes 1048576 | tf_op jit(solution)/shard_map/cond/branch_7_fun/reshape | solution.py:14
  129.6 19.5 %copy.75 = f32[2,2,2,128,128]{4,3,2,1,0:T(8,128)S(1)} copy(f32[2,2,2,128,128]{2,4,1,3,0:T(8,128)} %bitcast.141) | data formatting | bytes 1048576 | tf_op jit(solution)/shard_map/cond/branch_7_fun/transpose | solution.py:15
  149.1 1.1 copy.104
  153.1 0.0 all-to-all-done
  153.1 7.3 %all-to-all-start.1 = ((f32[8,32,512]{2,0,1:T(8,128)}), f32[8,32,512]{2,0,1:T(8,128)S(1)}, u32[]{:S(2)}, u32[]{:S(2)}) async-start(f32[8,32,512]{2,0,1:T(8,128)} %bitcast.34), calls=%async_computation.1 | async-start | bytes 1048576 | tf_op jit(solution)/shard_map/all_to_all | solution.py:50
  160.5 0.0 reduce-scatter.4.cloned.1.call-start
  160.5 1.1 bitcast_negate_fusion
  161.6 14.5 %all-to-all-done.1 = f32[8,32,512]{2,0,1:T(8,128)S(1)} async-done(((f32[8,32,512]{2,0,1:T(8,128)}), f32[8,32,512]{2,0,1:T(8,128)S(1)}, u32[]{:S(2)}, u32[]{:S(2)}) %all-to-all-start.1) | async-done | bytes 524320 | tf_op jit(solution)/shard_map/all_to_all | solution.py:50
  176.1 3.2 fusion
  179.3 1.0 copy.85
  180.3 0.0 reduce-scatter.4.cloned.1.call-update
  180.4 134.2 %reduce-scatter.4.cloned.1.call-done = f32[8,512]{1,0:T(8,128)} async-done(((f32[256,512]{1,0:T(8,128)}), f32[8,512]{1,0:T(8,128)}) %reduce-scatter.4.cloned.1.call-update) | async-done | bytes 16400
  314.6 0.8 copy.86
  315.5 0.7 copy.84
  316.2 0.7 copy.83
  (4 shorter events, 0.1 us)
Async XLA Ops:
  9.1 69.1 %copy-start = (f32[131072]{0:T(1024)S(1)}, f32[131072]{0:T(1024)}, u32[]{:S(2)}) copy-start(f32[131072]{0:T(1024)} %param.34) | copy-start | bytes 1572868
  78.2 74.9 %all-to-all-start = ((f32[8,32,512]{2,0,1:T(8,128)}), f32[8,32,512]{2,0,1:T(8,128)}, u32[]{:S(2)}, u32[]{:S(2)}) async-start(f32[8,32,512]{2,0,1:T(8,128)} %bitcast.31), calls=%async_computation | async-start | bytes 1048576 | tf_op jit(solution)/shard_map/all_to_all | solution.py:49
  153.1 23.0 %all-to-all-start.1 = ((f32[8,32,512]{2,0,1:T(8,128)}), f32[8,32,512]{2,0,1:T(8,128)S(1)}, u32[]{:S(2)}, u32[]{:S(2)}) async-start(f32[8,32,512]{2,0,1:T(8,128)} %bitcast.34), calls=%async_computation.1 | async-start | bytes 1048576 | tf_op jit(solution)/shard_map/all_to_all | solution.py:50
  160.5 154.1 %reduce-scatter.4.cloned.1.call-start = ((), (), s32[]{:S(2)}) async-start(), calls=%async_computation.3 | async-start | bytes 540672
Sparse Core Ops, SparseCore 0:
  180.5 134.0 reduce-scatter.3
where the time goes:
time: 329 us; the launch traced here: 324 us
  waiting for transfers between devices  149 us (45%)
  local copies, waits for them, and re-layouts  116 us (35%)
  loops' own time  24.9 us (8%)
  between operations  15.4 us (5%)
  starting transfers between devices  14.8 us (4%)
    unnamed x2, waiting for transfers between devices  134 us
    reshape x2, local copies, waits for them, and re-layouts, make_branch(): shaped = flat.reshape(2, upper, 2, lower, 2)  70.4 us
    transpose x2, local copies, waits for them, and re-layouts, make_branch(): moved = jnp.transpose(shaped, (0, 2, 4, 1, 3))  39 us
    all_to_all x1, waiting for transfers between devices, local(): lax.all_to_all(local_imag, 'dev', split_axis=1, concat_axis=0, tiled=True)  14.5 us
    another operation x1, loops' own time, local(): local_real = lax.switch(middle_place, branches, state_real)  12.9 us
    another operation x1, loops' own time, local(): local_imag = lax.switch(middle_place, branches, state_imag)  12 us
    all_to_all x1, starting transfers between devices, local(): lax.all_to_all(local_real, 'dev', split_axis=1, concat_axis=0, tiled=True)  7.46 us
    all_to_all x1, starting transfers between devices, local(): lax.all_to_all(local_imag, 'dev', split_axis=1, concat_axis=0, tiled=True)  7.33 us
  transfers between devices with their start and end apart: 3, of which 2 were waited for; matrix products, arithmetic and copies ran while one was open for 17% of the time, Pallas kernels for 0%

commit v1 on v0

--- a/solution.py
+++ b/solution.py
@@ -2,6 +2,12 @@
 import jax.numpy as jnp
 from jax import lax
 from jax.sharding import PartitionSpec as P
+
+
+def stacked_exchange(block, axis, split, join):
+    pieces = jnp.split(block, lax.axis_size(axis), axis=split)
+    got = lax.all_to_all(jnp.stack(pieces), axis, 0, 0)
+    return jnp.concatenate(got, axis=join)
 
 
 def regroup(local_bits):
@@ -47,7 +53,7 @@
     local_imag = lax.switch(middle_place, branches, state_imag)
     received_re, received_im = (
         lax.all_to_all(local_real, "dev", split_axis=1, concat_axis=0, tiled=True),
-        lax.all_to_all(local_imag, "dev", split_axis=1, concat_axis=0, tiled=True),
+        stacked_exchange(local_imag, "dev", 1, 0),
     )
     full_width = received_re.shape[0]
     scale = 1.0 / count_rest

time: 329 us -> 348 us (1.058)
  local copies, waits for them, and re-layouts: 116 us -> 135 us
    unnamed x6 -> x37, local copies, waits for them, and re-layouts: 3.18 us -> 21.8 us
  transfers between devices with their start and end apart: 3 -> 3, of which waited for: 2 -> 2; matrix products, arithmetic and copies ran while one was open for 17% -> 22% of each run, Pallas kernels for 0% -> 0%
where the time goes in v1:
time: 348 us; the launch traced here: 343 us
  waiting for transfers between devices  149 us (43%)
  local copies, waits for them, and re-layouts  135 us (39%)
  loops' own time  25.5 us (7%)
  between operations  15 us (4%)
  starting transfers between devices  14.8 us (4%)
    unnamed x2, waiting for transfers between devices  134 us
    reshape x2, local copies, waits for them, and re-layouts, make_branch(): shaped = flat.reshape(2, upper, 2, lower, 2)  70.5 us
    transpose x2, local copies, waits for them, and re-layouts, make_branch(): moved = jnp.transpose(shaped, (0, 2, 4, 1, 3))  39 us
    unnamed x37, local copies, waits for them, and re-layouts  21.8 us
    all_to_all x1, waiting for transfers between devices, stacked_exchange(): got = lax.all_to_all(jnp.stack(pieces), axis, 0, 0)  14.5 us
    another operation x1, loops' own time, local(): local_real = lax.switch(middle_place, branches, state_real)  13 us
    another operation x1, loops' own time, local(): local_imag = lax.switch(middle_place, branches, state_imag)  12.6 us
    all_to_all x1, starting transfers between devices, local(): lax.all_to_all(local_real, 'dev', split_axis=1, concat_axis=0, tiled=True)  7.46 us
  transfers between devices with their start and end apart: 3, of which 2 were waited for; matrix products, arithmetic and copies ran while one was open for 22% of the time, Pallas kernels for 0%

profile of v1, /device:TPU:0, one launch (start us, length us, event | category | flops | bytes accessed | tf_op | source)
XLA Modules:
  0.0 343.1 jit_solution(10182584299049835566)
XLA Ops:
  7.2 1.2 slice.15
  9.1 69.2 %conditional.2 = (f32[8,16384]{1,0:T(8,128)}) conditional(s32[]{:T(128)} %bitcast.510, f32[131072]{0:T(1024)} %param.33, f32[131072]{0:T(1024)} %param.33, f32[131072]{0:T(1024)} %param.33, f32[131072]{0:T(1024)} %param.33, f32[131072]{0:T(1024)} %param.33, f32[131072]{0:T(1024)} %param.33, ...), branch_computations={%region_0.1_spmd, %region_1.2_spmd, %region_2.3_spmd, %region_3.4_... | conditional | bytes 3145736 | solution.py:52
  17.4 35.6 %reshape.182 = f32[2,128,2,128,2]{4,3,2,1,0:T(8,128)} reshape(f32[131072]{0:T(1024)} %param.7) | data formatting | bytes 1048576 | tf_op jit(solution)/shard_map/cond/branch_7_fun/reshape | solution.py:20
  53.0 19.5 %copy.60 = f32[2,2,2,128,128]{4,3,2,1,0:T(8,128)S(1)} copy(f32[2,2,2,128,128]{2,4,1,3,0:T(8,128)} %bitcast.1084) | data formatting | bytes 1048576 | tf_op jit(solution)/shard_map/cond/branch_7_fun/transpose | solution.py:21
  72.5 1.1 copy.103
  78.3 7.5 %all-to-all-start = ((f32[8,32,512]{2,0,1:T(8,128)}), f32[8,32,512]{2,0,1:T(8,128)}, u32[]{:S(2)}, u32[]{:S(2)}) async-start(f32[8,32,512]{2,0,1:T(8,128)} %bitcast.511), calls=%async_computation | async-start | bytes 1048576 | tf_op jit(solution)/shard_map/all_to_all | solution.py:55
  85.8 67.3 %conditional.3 = (f32[1,8,512]{2,1,0:T(8,128)S(1)}, f32[1,8,512]{2,1,0:T(8,128)S(1)}, f32[1,8,512]{2,1,0:T(8,128)S(1)}, f32[1,8,512]{2,1,0:T(8,128)S(1)}, f32[1,...) conditional(s32[]{:T(128)} %bitcast.510, ...), branch_computations={%region_15.16_spmd, %region_16.17_spmd, %region_17.18_spmd, %regio... | conditional | bytes 4194560 | solution.py:53
  95.1 34.9 %reshape.212 = f32[2,128,2,128,2]{4,3,2,1,0:T(8,128)} reshape(f32[131072]{0:T(1024)S(1)} %param.22) | data formatting | bytes 1048576 | tf_op jit(solution)/shard_map/cond/branch_7_fun/reshape | solution.py:20
  129.9 19.5 %copy.75 = f32[2,2,2,128,128]{4,3,2,1,0:T(8,128)S(1)} copy(f32[2,2,2,128,128]{2,4,1,3,0:T(8,128)} %bitcast.1098) | data formatting | bytes 1048576 | tf_op jit(solution)/shard_map/cond/branch_7_fun/transpose | solution.py:21
  154.8 0.6 constant_dynamic-update-slice_fusion.28
  162.0 0.6 constant_dynamic-update-slice_fusion.16
  165.6 0.6 constant_dynamic-update-slice_fusion.10
  166.2 0.6 constant_dynamic-update-slice_fusion.9
  169.8 0.6 constant_dynamic-update-slice_fusion.3
  171.0 0.6 constant_dynamic-update-slice_fusion.1
  172.3 7.3 %all-to-all-start.1 = ((f32[32,8,512]{2,1,0:T(8,128)}), f32[32,8,512]{2,1,0:T(8,128)S(1)}, u32[]{:S(2)}, u32[]{:S(2)}) async-start(f32[32,8,512]{2,1,0:T(8,128)} %constant_dynamic-update-slice_fusion), calls=%async_computation.1 | async-start | bytes 1048576 | tf_op jit(solution)/shard_map/all_to_all | solution.py:9
  179.6 1.1 bitcast_negate_fusion
  180.7 14.5 %all-to-all-done.1 = f32[32,8,512]{2,1,0:T(8,128)S(1)} async-done(((f32[32,8,512]{2,1,0:T(8,128)}), f32[32,8,512]{2,1,0:T(8,128)S(1)}, u32[]{:S(2)}, u32[]{:S(2)}) %all-to-all-start.1) | async-done | bytes 524320 | tf_op jit(solution)/shard_map/all_to_all | solution.py:9
  195.2 3.2 fusion
  198.5 1.0 copy.85
  199.5 134.3 %reduce-scatter.4.cloned.1.call-done = f32[8,512]{1,0:T(8,128)} async-done(((f32[256,512]{1,0:T(8,128)}), f32[8,512]{1,0:T(8,128)}) %reduce-scatter.4.cloned.1.call-update) | async-done | bytes 16400
  333.8 0.8 copy.86
  334.7 0.7 copy.84
  335.4 0.7 copy.83
  (38 shorter events, 16.1 us)
Async XLA Ops:
  9.1 69.2 %copy-start = (f32[131072]{0:T(1024)S(1)}, f32[131072]{0:T(1024)}, u32[]{:S(2)}) copy-start(f32[131072]{0:T(1024)} %param.34) | copy-start | bytes 1572868
  78.3 94.0 %all-to-all-start = ((f32[8,32,512]{2,0,1:T(8,128)}), f32[8,32,512]{2,0,1:T(8,128)}, u32[]{:S(2)}, u32[]{:S(2)}) async-start(f32[8,32,512]{2,0,1:T(8,128)} %bitcast.511), calls=%async_computation | async-start | bytes 1048576 | tf_op jit(solution)/shard_map/all_to_all | solution.py:55
  172.3 22.9 %all-to-all-start.1 = ((f32[32,8,512]{2,1,0:T(8,128)}), f32[32,8,512]{2,1,0:T(8,128)S(1)}, u32[]{:S(2)}, u32[]{:S(2)}) async-start(f32[32,8,512]{2,1,0:T(8,128)} %constant_dynamic-update-slice_fusion), calls=%async_computation.1 | async-start | bytes 1048576 | tf_op jit(solution)/shard_map/all_to_all | solution.py:9
  179.6 154.2 %reduce-scatter.4.cloned.1.call-start = ((), (), s32[]{:S(2)}) async-start(), calls=%async_computation.3 | async-start | bytes 540672
Sparse Core Ops, SparseCore 0:
  199.6 134.1 reduce-scatter.3
